TPU v7x, 512 devices: a whole 4x4x16 slice. The times are simulated.
512 devices in a mesh: seq: 128 (over z, x, core), head: 4 (over y).
Axes of the slice: x: 4, y: 4, z: 16, core: 2. Of those that a mesh axis runs over, the one named last changes fastest.
Arguments:
- x_in: bfloat16 [32768, 5120], P('seq', 'head'), may hold values from -6 to 6
- bc_in: bfloat16 [32768, 256], P('seq'), may hold values from -6 to 6
- z_in: bfloat16 [32768, 5120], P('seq', 'head'), may hold values from -6 to 6
- dt_raw: float32 [80, 32768], P('head', 'seq'), may hold values from -3 to 3
- dt_bias: float32 [80], P('head'), may hold values from -2.8 to -1.7
- a_log: float32 [80], P('head'), as said below
- conv_x: float32 [4, 5120], P(None, 'head'), may hold values from -3 to 3
- conv_bc: float32 [4, 256], replicated, may hold values from -3 to 3
- conv_x_bias: float32 [5120], P('head'), may hold values from -3 to 3
- conv_bc_bias: float32 [256], replicated, may hold values from -3 to 3
- norm_weight: float32 [5120], P('head'), may hold values from 0.1 to 1.9
Outputs:
- y_out: bfloat16 [32768, 5120], P('seq', 'head')
Inputs may be any that keep to these rules, and one draw needn't show every extreme that they name: a_log is at least log(2 / 32768) and at most 0.
All inputs are finite; a program needn't handle non-finite values.
Results may differ from a plain program's by a relative error of at most 0.012.
Values may be sent and summed in bfloat16 or wider, within the bound.
A program may use at most 128 MiB of HBM per device.

v0:
```python
import jax
import jax.numpy as jnp
from jax import lax
from jax.sharding import Mesh
from jax.sharding import PartitionSpec as P

HEADS = 80
HEADDIM = 64
STATE = 128
CONV = 4
SPAN = 256
SEQ = ("seq_0", "seq_1", "seq_2")


def passed_along(value, axis, by):
    peers = lax.axis_size(axis)
    pairs = [(i, i + by) for i in range(peers) if 0 <= i + by < peers]
    return lax.ppermute(value, axis, pairs)


def neutral_like(value, identity):
    return jax.tree.map(
        lambda part, zero: jnp.zeros_like(part) + jnp.asarray(zero, part.dtype), value, identity
    )


def entering_2(value, axes, combine, identity):
    before = start = neutral_like(value, identity)
    subtotal = value
    for axis in reversed(axes):
        peers, place = (lax.axis_size(axis), lax.axis_index(axis))
        pieces = jax.tree.map(
            lambda part, kind: lax.all_gather(part.astype(kind), axis),
            subtotal,
            (jnp.bfloat16, jnp.bfloat16),
        )
        inside, subtotal = (start, start)
        for k in range(peers):
            passed = k < place
            subtotal = combine(
                subtotal, jax.tree.map(lambda part, own: part[k].astype(own.dtype), pieces, value)
            )
            inside = jax.tree.map(lambda new, old: jnp.where(passed, new, old), subtotal, inside)
        before = combine(inside, before)
    return before


def from_everyone(value, axis):
    peers = lax.axis_size(axis)
    return lax.all_to_all(
        jnp.broadcast_to(value[None], (peers, *value.shape)), axis, 0, 0, tiled=True
    )


def taken_together(value, axis):
    everything = from_everyone(value, axis)
    return jnp.sum(everything, axis=0)


def causal_conv(source, rim_rows, taps, conv_bias):
    tok_rows = source.shape[0]
    padded = jnp.concatenate([rim_rows, source], axis=0).astype(jnp.float32)
    running = conv_bias[None, :] + taps[0][None, :] * padded[0:tok_rows]
    for offset in range(1, taps.shape[0]):
        running = running + taps[offset][None, :] * padded[offset : offset + tok_rows]
    return jax.nn.silu(running).astype(jnp.bfloat16)


def span_terms(x_blk, b_blk, c_blk, step_blk, cumulative):
    length = c_blk.shape[0]
    scores = jnp.dot(c_blk, b_blk.T, preferred_element_type=jnp.float32)
    causal = jnp.arange(length)[:, None] >= jnp.arange(length)[None, :]
    log_gap = jnp.where(causal[None], cumulative[:, :, None] - cumulative[:, None, :], 0.0)
    mixing = jnp.where(
        causal[None], scores[None] * jnp.exp(log_gap) * step_blk[:, None, :], 0.0
    ).astype(jnp.bfloat16)
    y_inner = jnp.einsum("htj,jhp->thp", mixing, x_blk, preferred_element_type=jnp.float32)
    weight_in = jnp.exp(cumulative[:, -1:] - cumulative) * step_blk
    x_weighted = (x_blk.astype(jnp.float32) * weight_in.T[:, :, None]).astype(jnp.bfloat16)
    state_part = jnp.einsum("jhp,jn->hpn", x_weighted, b_blk, preferred_element_type=jnp.float32)
    return (y_inner, state_part)


def combine_carry(earlier, later):
    return (earlier[0] + later[0], jnp.exp(later[0])[:, None, None] * earlier[1] + later[1])


def local(
    x_in,
    bc_in,
    z_in,
    dt_raw,
    dt_bias,
    a_log,
    conv_x,
    conv_bc,
    conv_x_bias,
    conv_bc_bias,
    norm_weight,
):
    tok_rows = x_in.shape[0]
    head_count = dt_raw.shape[0]
    rim_width = CONV - 1
    x_rim, bc_rim = passed_along(
        (x_in[tok_rows - rim_width :], bc_in[tok_rows - rim_width :]), SEQ, 1
    )
    x_conv = causal_conv(x_in, x_rim, conv_x, conv_x_bias)
    bc_mixed = causal_conv(bc_in, bc_rim, conv_bc, conv_bc_bias)
    step_size = jax.nn.softplus(dt_raw + dt_bias[:, None])
    log_decay = step_size * (-jnp.exp(a_log))[:, None]
    span_count = tok_rows // SPAN
    x_blocks = x_conv.reshape(span_count, SPAN, head_count, HEADDIM)
    b_blocks = bc_mixed[:, :STATE].reshape(span_count, SPAN, STATE)
    c_blocks = bc_mixed[:, STATE:].reshape(span_count, SPAN, STATE)
    step_blocks = step_size.reshape(head_count, span_count, SPAN).transpose(1, 0, 2)
    decay_blocks = log_decay.reshape(head_count, span_count, SPAN).transpose(1, 0, 2)

    def local_span(carried, inputs):
        x_blk, b_blk, c_blk, step_blk, decay_blk = inputs
        cumulative = jnp.cumsum(decay_blk, axis=1)
        y_inner, state_part = span_terms(x_blk, b_blk, c_blk, step_blk, cumulative)
        updated = jnp.exp(cumulative[:, -1])[:, None, None] * carried + state_part
        return (updated, (y_inner, carried, cumulative))

    empty_state = jnp.zeros((head_count, HEADDIM, STATE), jnp.float32)
    local_state, (y_inner, before, cumulative) = lax.scan(
        local_span, empty_state, (x_blocks, b_blocks, c_blocks, step_blocks, decay_blocks)
    )
    span_decay = cumulative[:, :, -1]
    total_decay = jnp.sum(span_decay, axis=0)
    prior_decay = jnp.cumsum(span_decay, axis=0) - span_decay
    incoming_decay, incoming = entering_2(
        (total_decay, local_state),
        SEQ,
        combine_carry,
        (jnp.zeros((head_count,), jnp.float32), empty_state),
    )
    entering = jnp.exp(prior_decay)[:, :, None, None] * incoming[None] + before
    y_outer = jnp.einsum("ktn,khpn->kthp", c_blocks.astype(jnp.float32), entering)
    y_outer = y_outer * jnp.exp(cumulative).transpose(0, 2, 1)[:, :, :, None]
    y_full = (y_inner + y_outer).reshape(tok_rows, head_count * HEADDIM)
    gated_rows = y_full * jax.nn.silu(z_in.astype(jnp.float32))
    squares = jnp.sum(gated_rows * gated_rows, axis=1)
    whole_sum = taken_together(squares, "head")
    inv_rms = lax.rsqrt(whole_sum / (HEADS * HEADDIM) + 1e-05)
    return (gated_rows * inv_rms[:, None] * norm_weight[None, :]).astype(jnp.bfloat16)


def solution(mesh):
    torus = Mesh(
        mesh.devices.reshape(16, 4, 2, mesh.shape["head"]), ("seq_0", "seq_1", "seq_2", "head")
    )
    return jax.shard_map(
        local,
        mesh=torus,
        in_specs=(
            P(SEQ, "head"),
            P(SEQ, None),
            P(SEQ, "head"),
            P("head", SEQ),
            P("head"),
            P("head"),
            P(None, "head"),
            P(),
            P("head"),
            P(),
            P("head"),
        ),
        out_specs=P(SEQ, "head"),
        check_vma=False,
    )
```

profile of v0, /device:TPU:2, one launch (start us, length us, event | category | flops | bytes accessed | tf_op | source)
XLA Modules:
  0.0 171.6 jit_solution(9146427206971298142)
XLA Ops:
  6.5 0.8 slice.207
  7.4 0.3 copy.56
  7.6 1.9 %collective-permute-start = (bf16[3,1280]{0,1:T(8,128)(2,1)S(1)}, bf16[3,1280]{0,1:T(8,128)(2,1)S(1)}, u32[]{:S(2)}, u32[]{:S(2)}) collective-permute-start(bf16[3,1280]{0,1:T(8,128)(2,1)S(1)} %copy.56), channel_id=1, source_target_pairs={{0,4},{4,8},{8,12},{12,16},{16,20},{20,24},{24,28},{28,32},{32,36}... | collective-permute-start | bytes 23048 | tf_op jit(solution)/shard_map/ppermute | solution.py:18
  9.5 0.7 slice.216
  10.2 3.5 %collective-permute-start.1 = (bf16[3,256]{1,0:T(4,128)(2,1)S(1)}, bf16[3,256]{1,0:T(4,128)(2,1)S(1)}, u32[]{:S(2)}, u32[]{:S(2)}) collective-permute-start(bf16[3,256]{1,0:T(4,128)(2,1)S(1)} %slice.216), channel_id=1, source_target_pairs={{0,4},{4,8},{8,12},{12,16},{16,20},{20,24},{24,28},{28,32},{32,36}... | collective-permute-start | bytes 4616 | tf_op jit(solution)/shard_map/ppermute | solution.py:18
  13.7 0.7 exponential_negate_fusion
  14.4 0.8 broadcast_multiply_fusion
  15.3 0.6 reduce-window.6
  16.2 0.8 fusion.220
  17.2 1.8 %all-gather = bf16[2,20,1]{1,2,0:T(2,128)(2,1)S(1)} all-gather(bf16[1,20,1]{1,2,0:T(2,128)(2,1)S(1)} %get-tuple-element.72), channel_id=2, replica_groups=mesh['seq_0'=16,'seq_1'=4,'seq_2'=2,'head'=4] {'seq_2'}, dimensions={0}, use_global_device_ids=true | all-gather | bytes 120 | tf_op jit(solution)/shard_map/all_gather | solution.py:33
  19.3 0.9 slice_reduce_fusion.5
  20.3 0.2 copy.57
  20.6 0.2 multiply_convert_fusion.4
  20.8 0.4 maximum_convert_fusion
  21.3 0.2 copy-done.3
  21.5 2.2 %multiply_convert_fusion.2 = bf16[256,1280]{0,1:T(8,128)(2,1)S(1)} fusion(f32[259,1280]{0,1:T(8,128)S(1)} %maximum_convert_fusion, f32[1280]{0:T(1024)S(1)} %get-tuple-element.25, f32[1280]{0:T(1024)S(1)} %get-tuple-element.26, f32[1280]{0:T(1024)S(1)} %get-tuple-element.24, f32[1280]{0:T(1024)S(1)} %get-tuple-element.23, f32[1280]{0:T(1024)S(1)} %copy-done.3), kind=kLoop, calls=%fused_computation.28 | loop fusion | flops 4259840 | bytes 5923840 | tf_op jit(solution)/shard_map/convert_element_type | solution.py:66
  23.7 0.3 fusion.17
  24.1 2.3 %all-gather.1 = bf16[40,64,128]{2,1,0:T(8,128)(2,1)S(1)} all-gather(bf16[20,64,128]{2,1,0:T(8,128)(2,1)S(1)} %fusion.17), channel_id=3, replica_groups=mesh['seq_0'=16,'seq_1'=4,'seq_2'=2,'head'=4] {'seq_2'}, dimensions={0}, use_global_device_ids=true | all-gather | bytes 983040 | tf_op jit(solution)/shard_map/all_gather | solution.py:33
  26.3 1.0 fusion.97
  27.4 10.2 %all-gather.2 = bf16[4,1,20]{2,1,0:T(2,128)(2,1)S(1)} all-gather(bf16[1,1,20]{2,1,0:T(2,128)(2,1)S(1)} %get-tuple-element.69), channel_id=1, replica_groups=mesh['seq_0'=16,'seq_1'=4,'seq_2'=2,'head'=4] {'seq_1'}, dimensions={0}, use_global_device_ids=true | all-gather | bytes 200 | tf_op jit(solution)/shard_map/all_gather | solution.py:33
  37.6 25.7 %all-gather.7.cloned.1.call-done = bf16[4,20,64,128]{3,2,1,0:T(8,128)(2,1)} async-done(((bf16[1,20,64,128]{3,2,1,0:T(8,128)(2,1)}), bf16[4,20,64,128]{3,2,1,0:T(8,128)(2,1)}) %all-gather.7.cloned.1.call-update) | async-done | bytes 1310736 | tf_op jit(solution)/shard_map/all_gather | solution.py:33
  63.4 2.4 %fusion.95 = bf16[1,20,64,128]{3,2,1,0:T(8,128)(2,1)} fusion(f32[20]{0:T(128)S(1)} %get-tuple-element.67, f32[20]{0:T(128)S(1)} %get-tuple-element.66, f32[20]{0:T(128)S(1)} %get-tuple-element.65, f32[20]{0:T(128)S(1)} %get-tuple-element.64, bf16[4,20,64,128]{3,2,1,0:T(8,128)(2,1)} %all-gather.7.cloned.1.call-done), kind=kLoop, calls=%fused_computation.111 | loop fusion | flops 1966080 | bytes 1638720 | tf_op jit(solution)/shard_map/convert_element_type | solution.py:33
  65.8 0.2 copy.62
  66.1 30.3 %all-gather.3 = bf16[16,1,20]{2,1,0:T(2,128)(2,1)S(1)} all-gather(bf16[1,1,20]{2,1,0:T(2,128)(2,1)S(1)} %get-tuple-element.63), channel_id=1, replica_groups=mesh['seq_0'=16,'seq_1'=4,'seq_2'=2,'head'=4] {'seq_0'}, dimensions={0}, use_global_device_ids=true | all-gather | bytes 680 | tf_op jit(solution)/shard_map/all_gather | solution.py:33
  96.5 0.2 fusion.173
  96.7 2.8 %fusion.7 = f32[256,20,64]{0,2,1:T(8,128)} fusion(bf16[256,20,64]{0,2,1:T(8,128)(2,1)S(1)} %bitcast.132, f32[20,256]{1,0:T(8,128)S(1)} %get-tuple-element.40, f32[20,256]{1,0:T(8,128)S(1)} %bitcast.135, f32[256,256]{1,0:T(8,128)S(1)} %fusion.173, pred[256,256]{1,0:T(8,128)(4,1)S(1)} %iota_compare_fusion), kind=kOutput, calls=%fused_computation.10 | convolution fusion | flops 175636480 | bytes 2334720 | tf_op jit(solution)/shard_map/while/body/eval_jaxpr/htj,jhp->thp/dot_general | solution.py:77
  99.5 48.8 %all-gather.9.cloned.1.call-done = bf16[16,20,64,128]{3,2,1,0:T(8,128)(2,1)} async-done(((bf16[1,20,64,128]{3,2,1,0:T(8,128)(2,1)}), bf16[16,20,64,128]{3,2,1,0:T(8,128)(2,1)}) %all-gather.9.cloned.1.call-update) | async-done | bytes 5242896 | tf_op jit(solution)/shard_map/all_gather | solution.py:33
  148.3 5.0 %fusion.8 = f32[256,20,64]{0,2,1:T(8,128)S(1)} fusion(f32[256,20,64]{0,2,1:T(8,128)} %fusion.7, f32[256,20]{0,1:T(8,128)S(1)} %exponential_bitcast_fusion, bf16[16,20,64,128]{3,2,1,0:T(8,128)(2,1)} %all-gather.9.cloned.1.call-done, f32[20]{0:T(128)S(1)} %exponential_bitcast_fusion.5, f32[20]{0:T(128)S(1)} %get-tuple-element.70, ...), kind=kOutput, calls=%fused_computation.12 | convolution fusion | flops 99287040 | bytes 9933334 | tf_op jit(solution)/shard_map/ktn,khpn->kthp/dot_general | solution.py:139
  153.3 0.5 multiply_reduce_fusion
  153.7 9.4 %all_to_all.6 = f32[4,1,256]{2,1,0:T(1,128)S(1)} all-to-all(f32[4,1,256]{2,1,0:T(1,128)S(1)} %broadcast_in_dim.57), channel_id=1, replica_groups=mesh['seq_0'=16,'seq_1'=4,'seq_2'=2,'head'=4] {'head'}, dimensions={0} | all-to-all | bytes 8192 | tf_op jit(solution)/shard_map/all_to_all | solution.py:50
  163.2 0.5 multiply_convert_fusion
  163.6 1.1 copy.64
  (44 shorter events, 1.1 us)
Async XLA Ops:
  6.5 13.7 %copy-start = (bf16[256,1280]{1,0:T(8,128)(2,1)S(1)}, bf16[256,1280]{1,0:T(8,128)(2,1)}, u32[]{:S(2)}) copy-start(bf16[256,1280]{1,0:T(8,128)(2,1)} %param.11) | copy-start | bytes 1966084
  6.5 14.0 %copy-start.2 = (bf16[256,256]{1,0:T(8,128)(2,1)S(1)}, bf16[256,256]{1,0:T(8,128)(2,1)}, u32[]{:S(2)}) copy-start(bf16[256,256]{1,0:T(8,128)(2,1)} %param.12) | copy-start | bytes 393220
  6.5 56.8 %all-gather.7.cloned.1.call-start = ((), (), s32[]{:S(2)}) async-start(), calls=%async_computation.1 | async-start | bytes 1638400 | tf_op jit(solution)/shard_map/all_gather | solution.py:33
  7.3 13.2 %copy-start.5 = (f32[256]{0:T(256)S(1)}, f32[256]{0:T(256)}, u32[]{:S(2)}) copy-start(f32[256]{0:T(256)} %param.20) | copy-start | bytes 3076
  7.6 13.2 %collective-permute-start = (bf16[3,1280]{0,1:T(8,128)(2,1)S(1)}, bf16[3,1280]{0,1:T(8,128)(2,1)S(1)}, u32[]{:S(2)}, u32[]{:S(2)}) collective-permute-start(bf16[3,1280]{0,1:T(8,128)(2,1)S(1)} %copy.56), channel_id=1, source_target_pairs={{0,4},{4,8},{8,12},{12,16},{16,20},{20,24},{24,28},{28,32},{32,36}... | collective-permute-start | bytes 23048 | tf_op jit(solution)/shard_map/ppermute | solution.py:18
  10.2 10.3 %collective-permute-start.1 = (bf16[3,256]{1,0:T(4,128)(2,1)S(1)}, bf16[3,256]{1,0:T(4,128)(2,1)S(1)}, u32[]{:S(2)}, u32[]{:S(2)}) collective-permute-start(bf16[3,256]{1,0:T(4,128)(2,1)S(1)} %slice.216), channel_id=1, source_target_pairs={{0,4},{4,8},{8,12},{12,16},{16,20},{20,24},{24,28},{28,32},{32,36}... | collective-permute-start | bytes 4616 | tf_op jit(solution)/shard_map/ppermute | solution.py:18
  20.8 0.7 copy-start.3
  27.3 38.5 %copy-start.1 = (bf16[256,1280]{1,0:T(8,128)(2,1)S(1)}, bf16[256,1280]{1,0:T(8,128)(2,1)}, u32[]{:S(2)}) copy-start(bf16[256,1280]{1,0:T(8,128)(2,1)} %param.13) | copy-start | bytes 1966084
  27.4 120.9 %all-gather.9.cloned.1.call-start = ((), (), s32[]{:S(2)}) async-start(), calls=%async_computation.2 | async-start | bytes 5570560 | tf_op jit(solution)/shard_map/all_gather | solution.py:33
  153.3 9.9 %copy-start.4 = (f32[1280]{0:T(1024)S(1)}, f32[1280]{0:T(1024)}, u32[]{:S(2)}) copy-start(f32[1280]{0:T(1024)} %param.21) | copy-start | bytes 15364
Sparse Core Ops, SparseCore 0:
  27.5 35.8 all-gather.6
  65.9 82.3 all-gather.8
where the time goes:
time: 172 us
  waiting for transfers between devices  74.6 us (43%)
  blocking collectives  54 us (31%)
  between operations  13.7 us (8%)
  other arithmetic  9.61 us (6%)
  matrix products  8.25 us (5%)
  local copies, waits for them, and re-layouts  5.95 us (3%)
  starting transfers between devices  5.45 us (3%)
    all_gather x2, waiting for transfers between devices, entering_2(): lax.all_gather(part.astype(kind), axis)  74.6 us
    all_gather x4, blocking collectives, entering_2(): lax.all_gather(part.astype(kind), axis)  44.6 us
    all_to_all x1, blocking collectives, from_everyone(): lax.all_to_all(jnp.broadcast_to(value[None], (peers, *value.shape)), axis...  9.38 us
    ppermute x2, starting transfers between devices, passed_along(): return lax.ppermute(value, axis, pairs)  5.41 us
    dot_general x1, matrix products, local(): jnp.einsum('ktn,khpn->kthp', c_blocks.astype(jnp.float32), entering)  4.96 us
  transfers between devices with their start and end apart: 4, of which 2 were waited for; matrix products, arithmetic and copies ran while one was open for 5% of the time, Pallas kernels for 0%

commit v1 on v0

v1 whole, which is shorter than its diff:
```python
import functools

import jax
import jax.numpy as jnp
from jax import lax
from jax.experimental import pallas as pl
from jax.experimental.pallas import tpu as pltpu
from jax.sharding import Mesh
from jax.sharding import PartitionSpec as P

HEADDIM = 64
STATE = 128
CONV = 4
RIM = 16
GROUP = 3
EARLY_TILES = 6
AXES = ("seq_0", "seq_1", "seq_2", "head")
SEQ = AXES[:3]
F32 = jnp.float32
BF16 = jnp.bfloat16


def dot(a, b, contract=((1,), (0,)), precision=None):
    return lax.dot_general(
        a, b, (contract, ((), ())), preferred_element_type=F32, precision=precision
    )


def silu(value):
    return value / (1.0 + jnp.exp(-value))


def split_two(value):
    high = value.astype(BF16)
    low = (value - high.astype(F32)).astype(BF16)
    return jnp.concatenate([high, low], axis=1)


def split_three(value):
    high = value.astype(BF16)
    rest = value - high.astype(F32)
    mid = rest.astype(BF16)
    low = (rest - mid.astype(F32)).astype(BF16)
    return jnp.concatenate([high, mid, low], axis=1)


def layer_kernel(sizes, *refs):
    nz, nx, nc, ny, tok, heads, inner = sizes
    (
        x_hbm, bc_hbm, z_hbm, dt_hbm, bias_hbm, alog_hbm, cx_hbm, cbc_hbm, cxb_hbm, cbcb_hbm,
        nw_hbm, out_ref,
        x_v, bc_v, z_v, dt_v, bias_v, alog_v, cx_v, cbc_v, cxb_v, cbcb_v, nw_v,
        xrim, bcrim, xf, bcf, xc, xw, wrim, bmat_t, cmat, scores, dtp, smallp,
        cum_row, step_row, win2, ecum2, cum3, yg, eg, gz,
        stbuf, p1buf, dself, dbuf, pbuf, cumd, tbuf, dplane, abuf, adec,
        pst, fpre, qst, fall, ebuf, ech, obuf, ent, nself, nbuf,
        in_sem, rim_s, rim_r, p1s, p1r, d1s, d1r, as_, ar, ds_, dr, es, er, p3s, p3r, ns_, nr_,
    ) = refs
    tiles = inner // 128
    half = inner // 2
    plane = nx * nc
    rows = STATE // plane
    z = lax.axis_index("seq_0")
    x = lax.axis_index("seq_1")
    c = lax.axis_index("seq_2")
    y = lax.axis_index("head")
    k = x * nc + c
    zl = lax.rem(z, GROUP)

    def remote(source, target, send, recv, device):
        return pltpu.make_async_remote_copy(
            src_ref=source, dst_ref=target, send_sem=send, recv_sem=recv,
            device_id=device, device_id_type=pl.DeviceIdType.MESH,
        )

    def peer_in_plane(other):
        return (z, lax.div(other, nc), lax.rem(other, nc), y)

    def peer_along(other):
        return (other, x, c, y)

    def peer_head(other):
        return (z, x, c, other)

    last_in_plane = k == plane - 1
    first_in_plane = k == 0
    following = lax.rem(k + 1, plane)
    next_z = jnp.where(last_in_plane, z + 1, z)
    next_dev = (next_z, lax.div(following, nc), lax.rem(following, nc), y)
    gives_rim = jnp.logical_or(z < nz - 1, k < plane - 1)
    takes_rim = jnp.logical_or(z > 0, k > 0)
    reach = jnp.minimum(jnp.where(zl == 0, 2, jnp.where(zl == 1, 1, GROUP)), nz - 1 - z)

    with jax.named_scope("a_start"):
        pairs = (
            (x_hbm, x_v), (bc_hbm, bc_v), (dt_hbm, dt_v), (bias_hbm, bias_v), (alog_hbm, alog_v),
            (cx_hbm, cx_v), (cbc_hbm, cbc_v), (cxb_hbm, cxb_v), (cbcb_hbm, cbcb_v), (z_hbm, z_v),
            (nw_hbm, nw_v),
        )
        loads = [
            pltpu.make_async_copy(a, b if len(a.shape) > 1 else b.at[0], in_sem.at[i])
            for i, (a, b) in enumerate(pairs)
        ]
        for i in (2, 3, 4, 0, 5, 7, 1, 6, 8, 9, 10):
            loads[i].start()

        barrier = pltpu.get_barrier_semaphore()

        def greet(device):
            pl.semaphore_signal(
                barrier, inc=1, device_id=device, device_id_type=pl.DeviceIdType.MESH
            )

        for d in range(1, GROUP + 1):

            @pl.when(jnp.logical_and(zl >= d - 1, z >= d))
            def _():
                greet(peer_along(z - d))

        @pl.when(jnp.logical_and(first_in_plane, z > 0))
        def _():
            greet((z - 1, nx - 1, nc - 1, y))

        for d in range(1, plane):
            greet(peer_in_plane(lax.rem(k + d, plane)))
        for d in range(1, ny):
            greet(peer_head(lax.rem(y + d, ny)))
        dtp[...] = jnp.zeros_like(dtp)
        smallp[...] = jnp.zeros_like(smallp)
        xf[0:8, :] = jnp.zeros((8, inner), F32)
        for i in (2, 3, 4):
            loads[i].wait()

    with jax.named_scope("b_dt"):
        dtp[0:heads, :] = dt_v[...]
        smallp[0:1, 0:heads] = bias_v[...]
        smallp[8:9, 0:heads] = alog_v[...]
        raw = jnp.transpose(dtp[...]) + smallp[0:1, :]
        step_t = jnp.maximum(raw, 0.0) + jnp.log1p(jnp.exp(-jnp.abs(raw)))
        decay_t = step_t * (-jnp.exp(smallp[8:9, :]))
        tok_i = lax.broadcasted_iota(jnp.int32, (tok, tok), 0)
        tok_j = lax.broadcasted_iota(jnp.int32, (tok, tok), 1)
        causal = tok_i >= tok_j
        lower = jnp.where(causal, 1.0, 0.0).astype(F32)
        cum_t = dot(lower, decay_t, precision=lax.Precision.HIGHEST)
        cum_row[...] = jnp.transpose(cum_t)
        step_row[...] = jnp.transpose(step_t)
        total = cum_t[tok - 1 : tok, :]
        win2[...] = split_two(jnp.exp(total - cum_t) * step_t)
        ecum2[...] = split_two(jnp.exp(cum_t))
        cum3[...] = split_three(cum_t)
        dself[...] = jnp.broadcast_to(total, dself.shape)

    def spread(tile, depth):
        row = lax.broadcasted_iota(jnp.int32, (128 * depth, 128), 0)
        col = lax.broadcasted_iota(jnp.int32, (128 * depth, 128), 1)
        head = tile * 2 + lax.div(col, HEADDIM)
        return jnp.where(lax.rem(row, 128) == head, 1.0, 0.0).astype(BF16)

    def conv(source, count, taps, bias, lanes):
        running = bias[:, lanes] + taps[0:1, lanes] * source[5 : 5 + count, lanes]
        for offset in range(1, CONV):
            start = 5 + offset
            running = running + taps[offset : offset + 1, lanes] * source[start : start + count, lanes]
        return silu(running).astype(BF16)

    with jax.named_scope("c_conv"):
        for i in (0, 5, 7):
            loads[i].wait()

        def conv_tile(tile, carry):
            lanes = pl.ds(pl.multiple_of(tile * 128, 128), 128)
            xf[8 : 8 + tok, lanes] = x_v[:, lanes].astype(F32)
            x_tile = conv(xf, tok, cx_v, cxb_v, lanes)
            xc[:, lanes] = x_tile
            weight = dot(win2[...], spread(tile, 2))
            wrim[:, lanes] = weight[0:RIM, :]
            xw[:, lanes] = (x_tile.astype(F32) * weight).astype(BF16)
            return carry

        lax.fori_loop(0, tiles, conv_tile, 0, unroll=2)
        for i in (1, 6, 8):
            loads[i].wait()
        bcf[8 : 8 + tok, :] = bc_v[...].astype(F32)

    with jax.named_scope("d_barrier"):
        extra = jnp.where(jnp.logical_and(last_in_plane, z < nz - 1), 1, 0)
        pl.semaphore_wait(barrier, (plane - 1) + (ny - 1) + reach + extra)

    with jax.named_scope("e_rim"):
        rim_copies = [
            remote(x_v.at[pl.ds(tok - RIM, RIM), :], xrim, rim_s.at[0], rim_r.at[0], next_dev),
            remote(bc_v.at[pl.ds(tok - RIM, RIM), :], bcrim, rim_s.at[1], rim_r.at[1], next_dev),
        ]

        @pl.when(gives_rim)
        def _():
            for copy in rim_copies:
                copy.start()

        loads[9].wait()
        loads[10].wait()

        def gate_tile(tile, carry):
            lanes = pl.ds(pl.multiple_of(tile * 128, 128), 128)
            gate = silu(z_v[:, lanes].astype(F32))
            gz[:, lanes] = gate
            eg[:, lanes] = gate * dot(ecum2[...], spread(tile, 2))
            return carry

        lax.fori_loop(0, tiles, gate_tile, 0, unroll=2)

        @pl.when(takes_rim)
        def _():
            for copy in rim_copies:
                copy.wait_recv()
            xf[0:8, :] = xrim[...].astype(F32)[RIM - 8 :, :]
            bcf[0:8, :] = bcrim[...].astype(F32)[RIM - 8 :, :]

        @pl.when(jnp.logical_not(takes_rim))
        def _():
            xf[0:8, :] = jnp.zeros((8, inner), F32)
            bcf[0:8, :] = jnp.zeros((8, 2 * STATE), F32)

    with jax.named_scope("f_state"):
        b_conv = conv(bcf, tok, cbc_v, cbcb_v, slice(0, STATE))
        c_conv = conv(bcf, tok, cbc_v, cbcb_v, slice(STATE, 2 * STATE))
        cmat[...] = c_conv
        bmat_t[...] = jnp.transpose(b_conv.astype(F32)).astype(BF16)
        first = conv(xf, RIM, cx_v, cxb_v, slice(0, inner))
        xc[0:RIM, :] = first
        xw[0:RIM, :] = (first.astype(F32) * wrim[...]).astype(BF16)
        plane_copies = []
        for part in range(2):
            lanes = slice(part * half, part * half + half)
            state = dot(bmat_t[...], xw[:, lanes])
            stbuf[part] = state.reshape(plane, rows, half).astype(BF16)
            for d in range(1, plane):
                other = lax.rem(k + d, plane)
                device = peer_in_plane(other)
                copies = [
                    remote(
                        stbuf.at[part, other], p1buf.at[part, k],
                        p1s.at[part, d - 1], p1r.at[part, d - 1], device,
                    )
                ]
                if part == 0:
                    copies.append(
                        remote(dself, dbuf.at[k], d1s.at[d - 1], d1r.at[d - 1], device)
                    )
                for copy in copies:
                    copy.start()
                plane_copies += copies
            p1buf[part, pl.ds(k, 1)] = stbuf[part, pl.ds(k, 1)]
        dbuf[pl.ds(k, 1)] = dself[...][None]

    def inner_tile(tile, carry):
        lanes = pl.ds(pl.multiple_of(tile * 128, 128), 128)
        x_tile = xc[:, lanes]
        parts = []
        for side in range(2):
            head = tile * 2 + side
            row = lax.broadcasted_iota(jnp.int32, (384, tok), 0)
            pick = jnp.where(lax.rem(row, 128) == head, 1.0, 0.0).astype(BF16)
            column = dot(cum3[...], pick)
            gap = jnp.minimum(column - cum_row[pl.ds(head, 1), :], 0.0)
            mixing = (scores[...] * jnp.exp(gap) * step_row[pl.ds(head, 1), :]).astype(BF16)
            parts.append(dot(mixing, x_tile))
        lane = lax.broadcasted_iota(jnp.int32, (tok, 128), 1)
        yg[:, lanes] = jnp.where(lane < HEADDIM, parts[0], parts[1]) * gz[:, lanes]
        return carry

    with jax.named_scope("g_inner"):
        scores[...] = jnp.where(causal, dot(c_conv, b_conv, ((1,), (1,))), 0.0)
        split = EARLY_TILES
        lax.fori_loop(0, split, inner_tile, 0)

    with jax.named_scope("h_plane_wait"):
        for copy in plane_copies:
            copy.wait()

    with jax.named_scope("i_plane_scan"):
        spread_row = lax.broadcasted_iota(jnp.int32, (128, inner), 0)
        spread_col = lax.broadcasted_iota(jnp.int32, (128, inner), 1)
        spread_all = jnp.where(spread_row == lax.div(spread_col, HEADDIM), 1.0, 0.0).astype(F32)
        each = jnp.concatenate([dbuf[i, 0:1, :] for i in range(plane)], axis=0)
        before = [jnp.zeros((1, 128), F32)]
        for i in range(1, plane):
            before.append(before[-1] + each[i - 1 : i, :])
        whole = before[-1] + each[plane - 1 : plane, :]
        before = jnp.concatenate(before, axis=0)
        stacked = jnp.concatenate([each, before], axis=0)
        wide = dot(stacked, spread_all, precision=lax.Precision.HIGHEST)
        factor = jnp.exp(wide[0:plane, :])
        cumd[...] = jnp.exp(wide[plane : 2 * plane, :])
        dplane[...] = jnp.broadcast_to(whole, (8, 128))
        for part in range(2):
            lanes = slice(part * half, part * half + half)
            running = jnp.zeros((rows, half), F32)
            for i in range(plane):
                pbuf[i, :, lanes] = running
                running = factor[i : i + 1, lanes] * running + p1buf[part, i].astype(F32)
            tbuf[:, lanes] = running.astype(BF16)
            qst[:, lanes] = running

    def group_copies(slot, d):
        device = peer_along(z + d)
        return (
            remote(tbuf, abuf.at[slot], as_.at[d - 1], ar.at[slot], device),
            remote(dplane, adec.at[slot], ds_.at[d - 1], dr.at[slot], device),
        )

    group_sends = ((0, 2), (0, 1), (1, 1))

    def sends_group(slot, d):
        return jnp.logical_and(zl == slot, z + d < nz)

    with jax.named_scope("j_group_send"):
        for slot, d in group_sends:

            @pl.when(sends_group(slot, d))
            def _():
                for copy in group_copies(slot, d):
                    copy.start()

    with jax.named_scope("k_inner"):
        lax.fori_loop(split, tiles, inner_tile, 0)

    with jax.named_scope("l_group_wait"):

        @pl.when(zl == 0)
        def _():
            pst[...] = jnp.zeros_like(pst)
            fpre[...] = jnp.ones_like(fpre)

        def widened(row):
            return jnp.exp(dot(row, spread_all, precision=lax.Precision.HIGHEST))

        @pl.when(zl == 1)
        def _():
            for copy in group_copies(0, 1):
                copy.wait_recv()
            pst[...] = abuf[0].astype(F32)
            fpre[...] = widened(adec[0])

        @pl.when(zl == 2)
        def _():
            for slot in range(2):
                for copy in group_copies(slot, 1):
                    copy.wait_recv()
            mid = widened(adec[1])[0:1, :]
            own = widened(dplane[...])[0:1, :]
            prefix = mid * abuf[0].astype(F32) + abuf[1].astype(F32)
            pst[...] = prefix
            fpre[...] = widened(adec[0] + adec[1])
            qst[...] = own * prefix + qst[...]
            fall[...] = widened(adec[0] + adec[1] + dplane[...])

    def chain_copy(d):
        return remote(ebuf, ech, es.at[d - 1], er.at[0], peer_along(z + d))

    def sends_chain(d):
        return jnp.logical_and(zl == GROUP - 1, z + d < nz)

    with jax.named_scope("m_chain"):

        @pl.when(z < GROUP)
        def _():
            ech[...] = jnp.zeros_like(ech)

        @pl.when(z >= GROUP)
        def _():
            chain_copy(1).wait_recv()

        @pl.when(sends_chain(1))
        def _():
            ebuf[...] = (fall[0:1, :] * ech[...].astype(F32) + qst[...]).astype(BF16)

        for d in range(GROUP, 0, -1):

            @pl.when(sends_chain(d))
            def _():
                chain_copy(d).start()

    with jax.named_scope("n_back_send"):
        entering = fpre[0:1, :] * ech[...].astype(F32) + pst[...]
        own_rows = pl.ds(pl.multiple_of(k * rows, rows), rows)
        for i in range(plane):
            obuf[i] = (cumd[i : i + 1, :] * entering + pbuf[i]).astype(BF16)
        back = []
        for d in range(1, plane):
            other = lax.rem(k + d, plane)
            back.append(
                remote(
                    obuf.at[other], ent.at[own_rows, :], p3s.at[d - 1], p3r.at[d - 1],
                    peer_in_plane(other),
                )
            )
        for copy in back:
            copy.start()
        ent[own_rows, :] = obuf[pl.ds(k, 1)].reshape(rows, inner)

    with jax.named_scope("o_back_wait"):

        @pl.when(gives_rim)
        def _():
            for copy in rim_copies:
                copy.wait_send()

        for slot, d in group_sends:

            @pl.when(sends_group(slot, d))
            def _():
                for copy in group_copies(slot, d):
                    copy.wait_send()

        for copy in back:
            copy.wait()

    with jax.named_scope("p_outer"):
        squares = jnp.zeros((tok, 128), F32)
        for tile in range(tiles):
            lanes = slice(tile * 128, tile * 128 + 128)
            gated = yg[:, lanes] + eg[:, lanes] * dot(cmat[...], ent[:, lanes])
            yg[:, lanes] = gated
            squares = squares + gated * gated

    with jax.named_scope("q_norm"):
        nself[...] = dot(
            jnp.ones((8, 128), F32), squares, ((1,), (1,)), precision=lax.Precision.HIGHEST
        )
        shared = [
            remote(
                nself, nbuf.at[d - 1], ns_.at[d - 1], nr_.at[d - 1], peer_head(lax.rem(y + d, ny))
            )
            for d in range(1, ny)
        ]
        for copy in shared:
            copy.start()
        for d in range(GROUP, 0, -1):

            @pl.when(sends_chain(d))
            def _():
                chain_copy(d).wait_send()

        for copy in shared:
            copy.wait()
        summed = nself[...]
        for d in range(1, ny):
            summed = summed + nbuf[d - 1]
        inv = lax.rsqrt(summed / (ny * inner) + 1e-05)
        inv = jnp.transpose(jnp.concatenate([inv] * 16, axis=0))

    with jax.named_scope("r_out"):
        for tile in range(tiles):
            lanes = slice(tile * 128, tile * 128 + 128)
            out_ref[:, lanes] = (yg[:, lanes] * inv * nw_v[:, lanes]).astype(BF16)


def local(
    shape,
    x_in,
    bc_in,
    z_in,
    dt_raw,
    dt_bias,
    a_log,
    conv_x,
    conv_bc,
    conv_x_bias,
    conv_bc_bias,
    norm_weight,
):
    nz, nx, nc, ny = shape
    tok, inner = x_in.shape
    heads = dt_raw.shape[0]
    plane = nx * nc
    rows = STATE // plane
    half = inner // 2
    sizes = (nz, nx, nc, ny, tok, heads, inner)
    operands = (
        x_in, bc_in, z_in, dt_raw, dt_bias, a_log, conv_x, conv_bc, conv_x_bias, conv_bc_bias,
        norm_weight,
    )
    v = pltpu.VMEM
    dma = pltpu.SemaphoreType.DMA
    scratch = [v(o.shape if o.ndim > 1 else (1, *o.shape), o.dtype) for o in operands]
    others = max(ny - 1, 1)
    scratch += [
        v((RIM, inner), BF16), v((RIM, 2 * STATE), BF16),
        v((tok + 8, inner), F32), v((tok + 8, 2 * STATE), F32),
        v((tok, inner), BF16), v((tok, inner), BF16), v((RIM, inner), F32),
        v((STATE, tok), BF16), v((tok, STATE), BF16), v((tok, tok), F32),
        v((128, tok), F32), v((16, 128), F32),
        v((128, tok), F32), v((128, tok), F32), v((tok, 256), BF16), v((tok, 256), BF16),
        v((tok, 384), BF16), v((tok, inner), F32), v((tok, inner), F32), v((tok, inner), F32),
        v((2, plane, rows, half), BF16), v((2, plane, rows, half), BF16), v((8, 128), F32),
        v((plane, 8, 128), F32), v((plane, rows, inner), F32), v((plane, inner), F32),
        v((rows, inner), BF16), v((8, 128), F32), v((2, rows, inner), BF16), v((2, 8, 128), F32),
        v((rows, inner), F32), v((8, inner), F32), v((rows, inner), F32), v((8, inner), F32),
        v((rows, inner), BF16), v((rows, inner), BF16),
        v((plane, rows, inner), BF16), v((STATE, inner), BF16),
        v((8, tok), F32), v((others, 8, tok), F32),
        dma((11,)), dma((2,)), dma((2,)),
        dma((2, plane - 1)), dma((2, plane - 1)), dma((plane - 1,)), dma((plane - 1,)),
        dma((2,)), dma((2,)), dma((2,)), dma((2,)),
        dma((GROUP,)), dma((1,)),
        dma((plane - 1,)), dma((plane - 1,)), dma((others,)), dma((others,)),
    ]
    return pl.pallas_call(
        functools.partial(layer_kernel, sizes),
        out_shape=pltpu.VMEM((tok, inner), BF16),
        in_specs=[pl.BlockSpec(memory_space=pltpu.HBM)] * 11,
        out_specs=pl.BlockSpec(memory_space=pltpu.VMEM),
        scratch_shapes=scratch,
        compiler_params=pltpu.CompilerParams(
            collective_id=0, has_side_effects=True, vmem_limit_bytes=66000000
        ),
        name="layer",
    )(*operands)


def build(mesh, shape):
    torus = Mesh(mesh.devices.reshape(shape), AXES)
    return jax.shard_map(
        functools.partial(local, shape),
        mesh=torus,
        in_specs=(
            P(SEQ, "head"),
            P(SEQ, None),
            P(SEQ, "head"),
            P("head", SEQ),
            P("head"),
            P("head"),
            P(None, "head"),
            P(),
            P("head"),
            P(),
            P("head"),
        ),
        out_specs=P(SEQ, "head"),
        check_vma=False,
    )


def solution(mesh):
    return build(mesh, (16, 4, 2, mesh.shape["head"]))
```

time: 172 us -> 45.9 us (0.27)
  the two profiles are of different devices: /device:TPU:2 before, /device:TPU:480 now
where the time goes in v1:
time: 45.9 us; the launch traced here: 45.8 us
  Pallas kernels  45 us (98%)
  local copies, waits for them, and re-layouts  0.84 us (2%)
    pallas_call x1, Pallas kernels, local(): pl.pallas_call(functools.partial(layer_kernel, sizes), out_shape=pltpu.VM...  45 us

profile of v1, /device:TPU:480, one launch (start us, length us, event | category | flops | bytes accessed | tf_op | source)
XLA Modules:
  0.0 45.8 jit_solution(5367907786890631424)
XLA Ops:
  0.0 45.0 %layer.1 = bf16[256,1280]{1,0:T(8,128)(2,1)S(1)} custom-call(bf16[256,1280]{1,0:T(8,128)(2,1)} %refs_0_.1, bf16[256,256]{1,0:T(8,128)(2,1)} %refs_1_.1, bf16[256,1280]{1,0:T(8,128)(2,1)} %refs_2_.1, f32[20,256]{1,0:T(8,128)} %refs_3_.1, f32[20]{0:T(128)} %refs_4_.1, f32[20]{0:T(128)} %refs_5_.1, f32[4,1280]{1,0:T(4,128)} %refs_6_.1, f32[4,256]{1,0:T(4,128)} %refs_7_.1, ...), custom_call_target="tpu_custom_call" | custom-call | tf_op jit(solution)/shard_map/layer/pallas_call | solution.py:510
  45.0 0.8 %copy.13 = bf16[256,1280]{1,0:T(8,128)(2,1)} copy(bf16[256,1280]{1,0:T(8,128)(2,1)S(1)} %layer.1) | data formatting | bytes 1310720

commit v2 on v1

--- a/solution.py
+++ b/solution.py
@@ -14,6 +14,7 @@
 RIM = 16
 GROUP = 3
 EARLY_TILES = 6
+EARLY_CONV = 4
 AXES = ("seq_0", "seq_1", "seq_2", "head")
 SEQ = AXES[:3]
 F32 = jnp.float32
@@ -27,7 +28,8 @@
 
 
 def silu(value):
-    return value / (1.0 + jnp.exp(-value))
+    half = 0.5 * value
+    return half + half * jnp.tanh(half)
 
 
 def split_two(value):
@@ -55,6 +57,7 @@
         stbuf, p1buf, dself, dbuf, pbuf, cumd, tbuf, dplane, abuf, adec,
         pst, fpre, qst, fall, ebuf, ech, obuf, ent, nself, nbuf,
         in_sem, rim_s, rim_r, p1s, p1r, d1s, d1r, as_, ar, ds_, dr, es, er, p3s, p3r, ns_, nr_,
+        ready,
     ) = refs
     tiles = inner // 128
     half = inner // 2
@@ -65,7 +68,11 @@
     c = lax.axis_index("seq_2")
     y = lax.axis_index("head")
     k = x * nc + c
-    zl = lax.rem(z, GROUP)
+    groups = nz // GROUP
+    last_size = nz - GROUP * (groups - 1)
+    group = jnp.minimum(lax.div(z, GROUP), groups - 1)
+    zl = z - group * GROUP
+    hands_on = jnp.logical_and(zl == GROUP - 1, group < groups - 1)
 
     def remote(source, target, send, recv, device):
         return pltpu.make_async_remote_copy(
@@ -89,7 +96,12 @@
     next_dev = (next_z, lax.div(following, nc), lax.rem(following, nc), y)
     gives_rim = jnp.logical_or(z < nz - 1, k < plane - 1)
     takes_rim = jnp.logical_or(z > 0, k > 0)
-    reach = jnp.minimum(jnp.where(zl == 0, 2, jnp.where(zl == 1, 1, GROUP)), nz - 1 - z)
+    size = jnp.where(group == groups - 1, last_size, GROUP)
+    next_size = jnp.where(group == groups - 2, last_size, GROUP)
+    reach = jnp.where(hands_on, next_size, size - 1 - zl)
+
+    def has_source(d):
+        return jnp.logical_and(zl >= d - 1, z >= d)
 
     with jax.named_scope("a_start"):
         pairs = (
@@ -111,11 +123,11 @@
                 barrier, inc=1, device_id=device, device_id_type=pl.DeviceIdType.MESH
             )
 
-        for d in range(1, GROUP + 1):
-
-            @pl.when(jnp.logical_and(zl >= d - 1, z >= d))
-            def _():
-                greet(peer_along(z - d))
+        for d in range(1, last_size + 1):
+
+            @pl.when(d <= reach)
+            def _():
+                greet(peer_along(z + d))
 
         @pl.when(jnp.logical_and(first_in_plane, z > 0))
         def _():
@@ -178,14 +190,13 @@
             xw[:, lanes] = (x_tile.astype(F32) * weight).astype(BF16)
             return carry
 
-        lax.fori_loop(0, tiles, conv_tile, 0, unroll=2)
-        for i in (1, 6, 8):
-            loads[i].wait()
-        bcf[8 : 8 + tok, :] = bc_v[...].astype(F32)
+        lax.fori_loop(0, EARLY_CONV, conv_tile, 0, unroll=2)
+        loads[1].wait()
 
     with jax.named_scope("d_barrier"):
         extra = jnp.where(jnp.logical_and(last_in_plane, z < nz - 1), 1, 0)
-        pl.semaphore_wait(barrier, (plane - 1) + (ny - 1) + reach + extra)
+        sources = jnp.minimum(zl + 1, z)
+        pl.semaphore_wait(barrier, (plane - 1) + (ny - 1) + sources + extra)
 
     with jax.named_scope("e_rim"):
         rim_copies = [
@@ -198,17 +209,19 @@
             for copy in rim_copies:
                 copy.start()
 
-        loads[9].wait()
-        loads[10].wait()
-
-        def gate_tile(tile, carry):
-            lanes = pl.ds(pl.multiple_of(tile * 128, 128), 128)
-            gate = silu(z_v[:, lanes].astype(F32))
-            gz[:, lanes] = gate
-            eg[:, lanes] = gate * dot(ecum2[...], spread(tile, 2))
-            return carry
-
-        lax.fori_loop(0, tiles, gate_tile, 0, unroll=2)
+        for d in range(1, last_size + 1):
+
+            @pl.when(has_source(d))
+            def _():
+                pl.semaphore_signal(
+                    ready.at[d - 1], inc=1, device_id=peer_along(z - d),
+                    device_id_type=pl.DeviceIdType.MESH,
+                )
+
+        lax.fori_loop(EARLY_CONV, tiles, conv_tile, 0, unroll=2)
+        for i in (6, 8):
+            loads[i].wait()
+        bcf[8 : 8 + tok, :] = bc_v[...].astype(F32)
 
         @pl.when(takes_rim)
         def _():
@@ -271,6 +284,17 @@
         return carry
 
     with jax.named_scope("g_inner"):
+        loads[9].wait()
+        loads[10].wait()
+
+        def gate_tile(tile, carry):
+            lanes = pl.ds(pl.multiple_of(tile * 128, 128), 128)
+            gate = silu(z_v[:, lanes].astype(F32))
+            gz[:, lanes] = gate
+            eg[:, lanes] = gate * dot(ecum2[...], spread(tile, 2))
+            return carry
+
+        lax.fori_loop(0, tiles, gate_tile, 0, unroll=2)
         scores[...] = jnp.where(causal, dot(c_conv, b_conv, ((1,), (1,))), 0.0)
         split = EARLY_TILES
         lax.fori_loop(0, split, inner_tile, 0)
@@ -310,12 +334,18 @@
             remote(dplane, adec.at[slot], ds_.at[d - 1], dr.at[slot], device),
         )
 
-    group_sends = ((0, 2), (0, 1), (1, 1))
+    group_sends = [(i, d) for i in range(last_size - 1) for d in range(last_size - 1 - i, 0, -1)]
 
     def sends_group(slot, d):
-        return jnp.logical_and(zl == slot, z + d < nz)
+        return jnp.logical_and(zl == slot, zl + d < size)
 
     with jax.named_scope("j_group_send"):
+        for d in range(1, last_size + 1):
+
+            @pl.when(d <= reach)
+            def _():
+                pl.semaphore_wait(ready.at[d - 1], 1)
+
         for slot, d in group_sends:
 
             @pl.when(sends_group(slot, d))
@@ -323,9 +353,6 @@
                 for copy in group_copies(slot, d):
                     copy.start()
 
-    with jax.named_scope("k_inner"):
-        lax.fori_loop(split, tiles, inner_tile, 0)
-
     with jax.named_scope("l_group_wait"):
 
         @pl.when(zl == 0)
@@ -336,31 +363,29 @@
         def widened(row):
             return jnp.exp(dot(row, spread_all, precision=lax.Precision.HIGHEST))
 
-        @pl.when(zl == 1)
-        def _():
-            for copy in group_copies(0, 1):
-                copy.wait_recv()
-            pst[...] = abuf[0].astype(F32)
-            fpre[...] = widened(adec[0])
-
-        @pl.when(zl == 2)
-        def _():
-            for slot in range(2):
-                for copy in group_copies(slot, 1):
-                    copy.wait_recv()
-            mid = widened(adec[1])[0:1, :]
-            own = widened(dplane[...])[0:1, :]
-            prefix = mid * abuf[0].astype(F32) + abuf[1].astype(F32)
-            pst[...] = prefix
-            fpre[...] = widened(adec[0] + adec[1])
-            qst[...] = own * prefix + qst[...]
-            fall[...] = widened(adec[0] + adec[1] + dplane[...])
+        for place in range(1, last_size):
+
+            @pl.when(zl == place)
+            def _():
+                for slot in range(place):
+                    for copy in group_copies(slot, 1):
+                        copy.wait_recv()
+                prefix = abuf[0].astype(F32)
+                decay = adec[0]
+                for slot in range(1, place):
+                    prefix = widened(adec[slot])[0:1, :] * prefix + abuf[slot].astype(F32)
+                    decay = decay + adec[slot]
+                pst[...] = prefix
+                fpre[...] = widened(decay)
+                if place == GROUP - 1:
+                    qst[...] = widened(dplane[...])[0:1, :] * prefix + qst[...]
+                    fall[...] = widened(decay + dplane[...])
 
     def chain_copy(d):
         return remote(ebuf, ech, es.at[d - 1], er.at[0], peer_along(z + d))
 
     def sends_chain(d):
-        return jnp.logical_and(zl == GROUP - 1, z + d < nz)
+        return jnp.logical_and(hands_on, d <= next_size)
 
     with jax.named_scope("m_chain"):
 
@@ -376,7 +401,7 @@
         def _():
             ebuf[...] = (fall[0:1, :] * ech[...].astype(F32) + qst[...]).astype(BF16)
 
-        for d in range(GROUP, 0, -1):
+        for d in range(last_size, 0, -1):
 
             @pl.when(sends_chain(d))
             def _():
@@ -400,6 +425,9 @@
             copy.start()
         ent[own_rows, :] = obuf[pl.ds(k, 1)].reshape(rows, inner)
 
+    with jax.named_scope("n_inner"):
+        lax.fori_loop(split, tiles, inner_tile, 0)
+
     with jax.named_scope("o_back_wait"):
 
         @pl.when(gives_rim)
@@ -437,7 +465,7 @@
         ]
         for copy in shared:
             copy.start()
-        for d in range(GROUP, 0, -1):
+        for d in range(last_size, 0, -1):
 
             @pl.when(sends_chain(d))
             def _():
@@ -486,6 +514,7 @@
     dma = pltpu.SemaphoreType.DMA
     scratch = [v(o.shape if o.ndim > 1 else (1, *o.shape), o.dtype) for o in operands]
     others = max(ny - 1, 1)
+    last = nz - GROUP * (nz // GROUP - 1)
     scratch += [
         v((RIM, inner), BF16), v((RIM, 2 * STATE), BF16),
         v((tok + 8, inner), F32), v((tok + 8, 2 * STATE), F32),
@@ -496,16 +525,18 @@
         v((tok, 384), BF16), v((tok, inner), F32), v((tok, inner), F32), v((tok, inner), F32),
         v((2, plane, rows, half), BF16), v((2, plane, rows, half), BF16), v((8, 128), F32),
         v((plane, 8, 128), F32), v((plane, rows, inner), F32), v((plane, inner), F32),
-        v((rows, inner), BF16), v((8, 128), F32), v((2, rows, inner), BF16), v((2, 8, 128), F32),
+        v((rows, inner), BF16), v((8, 128), F32), v((last - 1, rows, inner), BF16),
+        v((last - 1, 8, 128), F32),
         v((rows, inner), F32), v((8, inner), F32), v((rows, inner), F32), v((8, inner), F32),
         v((rows, inner), BF16), v((rows, inner), BF16),
         v((plane, rows, inner), BF16), v((STATE, inner), BF16),
         v((8, tok), F32), v((others, 8, tok), F32),
         dma((11,)), dma((2,)), dma((2,)),
         dma((2, plane - 1)), dma((2, plane - 1)), dma((plane - 1,)), dma((plane - 1,)),
-        dma((2,)), dma((2,)), dma((2,)), dma((2,)),
-        dma((GROUP,)), dma((1,)),
+        dma((last - 1,)), dma((last - 1,)), dma((last - 1,)), dma((last - 1,)),
+        dma((last,)), dma((1,)),
         dma((plane - 1,)), dma((plane - 1,)), dma((others,)), dma((others,)),
+        pltpu.SemaphoreType.REGULAR((last,)),
     ]
     return pl.pallas_call(
         functools.partial(layer_kernel, sizes),

time: 45.9 us -> 41.6 us (0.906)
  Pallas kernels: 45 us -> 40.6 us
    pallas_call x1, Pallas kernels: 45 us -> 40.6 us  [local(): pl.pallas_call(functools.partial(layer_kernel, sizes), out_shape=pltpu.VM...]
where the time goes in v2:
time: 41.6 us; the launch traced here: 41.5 us
  Pallas kernels  40.6 us (98%)
  local copies, waits for them, and re-layouts  0.84 us (2%)
    pallas_call x1, Pallas kernels, local(): pl.pallas_call(functools.partial(layer_kernel, sizes), out_shape=pltpu.VM...  40.6 us
    unnamed x1, local copies, waits for them, and re-layouts  0.84 us

profile of v2, /device:TPU:480, one launch (start us, length us, event | category | flops | bytes accessed | tf_op | source)
XLA Modules:
  0.0 41.5 jit_solution(17524846397879488711)
XLA Ops:
  0.0 40.6 %layer.1 = bf16[256,1280]{1,0:T(8,128)(2,1)S(1)} custom-call(bf16[256,1280]{1,0:T(8,128)(2,1)} %refs_0_.1, bf16[256,256]{1,0:T(8,128)(2,1)} %refs_1_.1, bf16[256,1280]{1,0:T(8,128)(2,1)} %refs_2_.1, f32[20,256]{1,0:T(8,128)} %refs_3_.1, f32[20]{0:T(128)} %refs_4_.1, f32[20]{0:T(128)} %refs_5_.1, f32[4,1280]{1,0:T(4,128)} %refs_6_.1, f32[4,256]{1,0:T(4,128)} %refs_7_.1, ...), custom_call_target="tpu_custom_call" | custom-call | tf_op jit(solution)/shard_map/layer/pallas_call | solution.py:541
  40.6 0.8 %copy.13 = bf16[256,1280]{1,0:T(8,128)(2,1)} copy(bf16[256,1280]{1,0:T(8,128)(2,1)S(1)} %layer.1) | data formatting | bytes 1310720

commit v3 on v2

--- a/solution.py
+++ b/solution.py
@@ -62,12 +62,13 @@
     tiles = inner // 128
     half = inner // 2
     plane = nx * nc
-    rows = STATE // plane
+    rows = STATE // nx
     z = lax.axis_index("seq_0")
     x = lax.axis_index("seq_1")
     c = lax.axis_index("seq_2")
     y = lax.axis_index("head")
     k = x * nc + c
+    owner = c == nc - 1
     groups = nz // GROUP
     last_size = nz - GROUP * (groups - 1)
     group = jnp.minimum(lax.div(z, GROUP), groups - 1)
@@ -82,6 +83,12 @@
 
     def peer_in_plane(other):
         return (z, lax.div(other, nc), lax.rem(other, nc), y)
+
+    def owner_of(other):
+        return (z, other, nc - 1, y)
+
+    def owner_lane(shift):
+        return lax.rem(x + shift, nx)
 
     def peer_along(other):
         return (other, x, c, y)
@@ -125,7 +132,7 @@
 
         for d in range(1, last_size + 1):
 
-            @pl.when(d <= reach)
+            @pl.when(jnp.logical_and(owner, d <= reach))
             def _():
                 greet(peer_along(z + d))
 
@@ -133,8 +140,16 @@
         def _():
             greet((z - 1, nx - 1, nc - 1, y))
 
-        for d in range(1, plane):
-            greet(peer_in_plane(lax.rem(k + d, plane)))
+        @pl.when(owner)
+        def _():
+            for d in range(1, plane):
+                greet(peer_in_plane(lax.rem(k + d, plane)))
+
+        @pl.when(jnp.logical_not(owner))
+        def _():
+            for shift in range(nx):
+                greet(owner_of(owner_lane(shift)))
+
         for d in range(1, ny):
             greet(peer_head(lax.rem(y + d, ny)))
         dtp[...] = jnp.zeros_like(dtp)
@@ -195,8 +210,8 @@
 
     with jax.named_scope("d_barrier"):
         extra = jnp.where(jnp.logical_and(last_in_plane, z < nz - 1), 1, 0)
-        sources = jnp.minimum(zl + 1, z)
-        pl.semaphore_wait(barrier, (plane - 1) + (ny - 1) + sources + extra)
+        near = jnp.where(owner, plane - 1 + jnp.minimum(zl + 1, z), nx)
+        pl.semaphore_wait(barrier, near + (ny - 1) + extra)
 
     with jax.named_scope("e_rim"):
         rim_copies = [
@@ -211,7 +226,7 @@
 
         for d in range(1, last_size + 1):
 
-            @pl.when(has_source(d))
+            @pl.when(jnp.logical_and(owner, has_source(d)))
             def _():
                 pl.semaphore_signal(
                     ready.at[d - 1], inc=1, device_id=peer_along(z - d),
@@ -243,29 +258,39 @@
         first = conv(xf, RIM, cx_v, cxb_v, slice(0, inner))
         xc[0:RIM, :] = first
         xw[0:RIM, :] = (first.astype(F32) * wrim[...]).astype(BF16)
-        plane_copies = []
+
+        def to_owner(part, shift):
+            lane = owner_lane(shift)
+            return remote(
+                stbuf.at[part, lane], p1buf.at[part, k], p1s.at[part, shift], p1r.at[part, k],
+                owner_of(lane),
+            )
+
+        def decay_to_owner(shift):
+            return remote(dself, dbuf.at[k], d1s.at[shift], d1r.at[k], owner_of(owner_lane(shift)))
+
         for part in range(2):
             lanes = slice(part * half, part * half + half)
             state = dot(bmat_t[...], xw[:, lanes])
-            stbuf[part] = state.reshape(plane, rows, half).astype(BF16)
-            for d in range(1, plane):
-                other = lax.rem(k + d, plane)
-                device = peer_in_plane(other)
-                copies = [
-                    remote(
-                        stbuf.at[part, other], p1buf.at[part, k],
-                        p1s.at[part, d - 1], p1r.at[part, d - 1], device,
-                    )
-                ]
+            stbuf[part] = state.reshape(nx, rows, half).astype(BF16)
+            for shift in range(1, nx):
                 if part == 0:
-                    copies.append(
-                        remote(dself, dbuf.at[k], d1s.at[d - 1], d1r.at[d - 1], device)
-                    )
-                for copy in copies:
-                    copy.start()
-                plane_copies += copies
-            p1buf[part, pl.ds(k, 1)] = stbuf[part, pl.ds(k, 1)]
-        dbuf[pl.ds(k, 1)] = dself[...][None]
+                    decay_to_owner(shift).start()
+                to_owner(part, shift).start()
+
+            @pl.when(jnp.logical_not(owner))
+            def _():
+                if part == 0:
+                    decay_to_owner(0).start()
+                to_owner(part, 0).start()
+
+            @pl.when(owner)
+            def _():
+                p1buf[part, pl.ds(k, 1)] = stbuf[part, pl.ds(x, 1)]
+
+        @pl.when(owner)
+        def _():
+            dbuf[pl.ds(k, 1)] = dself[...][None]
 
     def inner_tile(tile, carry):
         lanes = pl.ds(pl.multiple_of(tile * 128, 128), 128)
@@ -299,33 +324,12 @@
         split = EARLY_TILES
         lax.fori_loop(0, split, inner_tile, 0)
 
-    with jax.named_scope("h_plane_wait"):
-        for copy in plane_copies:
-            copy.wait()
-
-    with jax.named_scope("i_plane_scan"):
-        spread_row = lax.broadcasted_iota(jnp.int32, (128, inner), 0)
-        spread_col = lax.broadcasted_iota(jnp.int32, (128, inner), 1)
-        spread_all = jnp.where(spread_row == lax.div(spread_col, HEADDIM), 1.0, 0.0).astype(F32)
-        each = jnp.concatenate([dbuf[i, 0:1, :] for i in range(plane)], axis=0)
-        before = [jnp.zeros((1, 128), F32)]
-        for i in range(1, plane):
-            before.append(before[-1] + each[i - 1 : i, :])
-        whole = before[-1] + each[plane - 1 : plane, :]
-        before = jnp.concatenate(before, axis=0)
-        stacked = jnp.concatenate([each, before], axis=0)
-        wide = dot(stacked, spread_all, precision=lax.Precision.HIGHEST)
-        factor = jnp.exp(wide[0:plane, :])
-        cumd[...] = jnp.exp(wide[plane : 2 * plane, :])
-        dplane[...] = jnp.broadcast_to(whole, (8, 128))
-        for part in range(2):
-            lanes = slice(part * half, part * half + half)
-            running = jnp.zeros((rows, half), F32)
-            for i in range(plane):
-                pbuf[i, :, lanes] = running
-                running = factor[i : i + 1, lanes] * running + p1buf[part, i].astype(F32)
-            tbuf[:, lanes] = running.astype(BF16)
-            qst[:, lanes] = running
+    spread_row = lax.broadcasted_iota(jnp.int32, (128, inner), 0)
+    spread_col = lax.broadcasted_iota(jnp.int32, (128, inner), 1)
+    spread_all = jnp.where(spread_row == lax.div(spread_col, HEADDIM), 1.0, 0.0).astype(F32)
+
+    def widened(row):
+        return jnp.exp(dot(row, spread_all, precision=lax.Precision.HIGHEST))
 
     def group_copies(slot, d):
         device = peer_along(z + d)
@@ -339,91 +343,142 @@
     def sends_group(slot, d):
         return jnp.logical_and(zl == slot, zl + d < size)
 
-    with jax.named_scope("j_group_send"):
-        for d in range(1, last_size + 1):
-
-            @pl.when(d <= reach)
-            def _():
-                pl.semaphore_wait(ready.at[d - 1], 1)
-
-        for slot, d in group_sends:
-
-            @pl.when(sends_group(slot, d))
-            def _():
-                for copy in group_copies(slot, d):
-                    copy.start()
-
-    with jax.named_scope("l_group_wait"):
-
-        @pl.when(zl == 0)
-        def _():
-            pst[...] = jnp.zeros_like(pst)
-            fpre[...] = jnp.ones_like(fpre)
-
-        def widened(row):
-            return jnp.exp(dot(row, spread_all, precision=lax.Precision.HIGHEST))
-
-        for place in range(1, last_size):
-
-            @pl.when(zl == place)
-            def _():
-                for slot in range(place):
-                    for copy in group_copies(slot, 1):
-                        copy.wait_recv()
-                prefix = abuf[0].astype(F32)
-                decay = adec[0]
-                for slot in range(1, place):
-                    prefix = widened(adec[slot])[0:1, :] * prefix + abuf[slot].astype(F32)
-                    decay = decay + adec[slot]
-                pst[...] = prefix
-                fpre[...] = widened(decay)
-                if place == GROUP - 1:
-                    qst[...] = widened(dplane[...])[0:1, :] * prefix + qst[...]
-                    fall[...] = widened(decay + dplane[...])
-
-    def chain_copy(d):
-        return remote(ebuf, ech, es.at[d - 1], er.at[0], peer_along(z + d))
+    def chain_copy(part, d):
+        return remote(
+            ebuf.at[part], ech.at[part], es.at[part, d - 1], er.at[part], peer_along(z + d)
+        )
 
     def sends_chain(d):
         return jnp.logical_and(hands_on, d <= next_size)
 
-    with jax.named_scope("m_chain"):
-
-        @pl.when(z < GROUP)
-        def _():
-            ech[...] = jnp.zeros_like(ech)
-
-        @pl.when(z >= GROUP)
-        def _():
-            chain_copy(1).wait_recv()
-
-        @pl.when(sends_chain(1))
-        def _():
-            ebuf[...] = (fall[0:1, :] * ech[...].astype(F32) + qst[...]).astype(BF16)
-
-        for d in range(last_size, 0, -1):
-
-            @pl.when(sends_chain(d))
+    own_rows = pl.ds(pl.multiple_of(x * rows, rows), rows)
+
+    def back_copy(part, d):
+        other = lax.rem(k + d, plane)
+        return remote(
+            obuf.at[part, other], ent.at[part, own_rows, :], p3s.at[part, d - 1], p3r.at[part, x],
+            peer_in_plane(other),
+        )
+
+    def back_from(part, shift):
+        lane = owner_lane(shift)
+        return remote(
+            obuf.at[part, 0], ent.at[part, own_rows, :], p3s.at[part, 0], p3r.at[part, lane],
+            owner_of(lane),
+        )
+
+    @pl.when(owner)
+    def _():
+        with jax.named_scope("h_plane_wait"):
+            for d in range(1, plane):
+                source = lax.rem(k + d, plane)
+                remote(
+                    dself, dbuf.at[source], d1s.at[0], d1r.at[source], peer_in_plane(source)
+                ).wait_recv()
+                for part in range(2):
+                    remote(
+                        stbuf.at[part, 0], p1buf.at[part, source], p1s.at[part, 0],
+                        p1r.at[part, source], peer_in_plane(source),
+                    ).wait_recv()
+
+        with jax.named_scope("i_plane_scan"):
+            each = jnp.concatenate([dbuf[i, 0:1, :] for i in range(plane)], axis=0)
+            before = [jnp.zeros((1, 128), F32)]
+            for i in range(1, plane):
+                before.append(before[-1] + each[i - 1 : i, :])
+            whole = before[-1] + each[plane - 1 : plane, :]
+            before = jnp.concatenate(before, axis=0)
+            wide = widened(jnp.concatenate([each, before], axis=0))
+            factor = wide[0:plane, :]
+            cumd[...] = wide[plane : 2 * plane, :]
+            dplane[...] = jnp.broadcast_to(whole, (8, 128))
+            for part in range(2):
+                lanes = slice(part * half, part * half + half)
+                running = jnp.zeros((rows, half), F32)
+                for i in range(plane):
+                    pbuf[i, :, lanes] = running
+                    running = factor[i : i + 1, lanes] * running + p1buf[part, i].astype(F32)
+                tbuf[:, lanes] = running.astype(BF16)
+                qst[:, lanes] = running
+
+        with jax.named_scope("j_group_send"):
+            for d in range(1, last_size + 1):
+
+                @pl.when(d <= reach)
+                def _():
+                    pl.semaphore_wait(ready.at[d - 1], 1)
+
+            for slot, d in group_sends:
+
+                @pl.when(sends_group(slot, d))
+                def _():
+                    for copy in group_copies(slot, d):
+                        copy.start()
+
+        with jax.named_scope("l_group_wait"):
+
+            @pl.when(zl == 0)
             def _():
-                chain_copy(d).start()
-
-    with jax.named_scope("n_back_send"):
-        entering = fpre[0:1, :] * ech[...].astype(F32) + pst[...]
-        own_rows = pl.ds(pl.multiple_of(k * rows, rows), rows)
-        for i in range(plane):
-            obuf[i] = (cumd[i : i + 1, :] * entering + pbuf[i]).astype(BF16)
-        back = []
-        for d in range(1, plane):
-            other = lax.rem(k + d, plane)
-            back.append(
-                remote(
-                    obuf.at[other], ent.at[own_rows, :], p3s.at[d - 1], p3r.at[d - 1],
-                    peer_in_plane(other),
-                )
-            )
-        for copy in back:
-            copy.start()
-        ent[own_rows, :] = obuf[pl.ds(k, 1)].reshape(rows, inner)
+                pst[...] = jnp.zeros_like(pst)
+                fpre[...] = jnp.ones_like(fpre)
+
+            for place in range(1, last_size):
+
+                @pl.when(zl == place)
+                def _():
+                    for slot in range(place):
+                        for copy in group_copies(slot, 1):
+                            copy.wait_recv()
+                    prefix = abuf[0].astype(F32)
+                    decay = adec[0]
+                    for slot in range(1, place):
+                        prefix = widened(adec[slot])[0:1, :] * prefix + abuf[slot].astype(F32)
+                        decay = decay + adec[slot]
+                    pst[...] = prefix
+                    fpre[...] = widened(decay)
+                    if place == GROUP - 1:
+                        qst[...] = widened(dplane[...])[0:1, :] * prefix + qst[...]
+                        fall[...] = widened(decay + dplane[...])
+
+        for part in range(2):
+            lanes = slice(part * half, part * half + half)
+            with jax.named_scope("m_chain"):
+
+                @pl.when(group == 0)
+                def _():
+                    ech[part] = jnp.zeros((rows, half), BF16)
+
+                @pl.when(group > 0)
+                def _():
+                    chain_copy(part, 1).wait_recv()
+
+                @pl.when(hands_on)
+                def _():
+                    ebuf[part] = (
+                        fall[0:1, lanes] * ech[part].astype(F32) + qst[:, lanes]
+                    ).astype(BF16)
+                    chain_copy(part, GROUP).start()
+
+        with jax.named_scope("m_hand_on"):
+            for d in range(last_size, 0, -1):
+                if d != GROUP:
+
+                    @pl.when(sends_chain(d))
+                    def _():
+                        for part in range(2):
+                            chain_copy(part, d).start()
+
+        with jax.named_scope("n_back_send"):
+            for part in range(2):
+                lanes = slice(part * half, part * half + half)
+                entering = fpre[0:1, lanes] * ech[part].astype(F32) + pst[:, lanes]
+                for i in range(plane):
+                    obuf[part, i] = (
+                        cumd[i : i + 1, lanes] * entering + pbuf[i, :, lanes]
+                    ).astype(BF16)
+                for d in range(1, plane):
+                    back_copy(part, d).start()
+                ent[part, own_rows, :] = obuf[part, pl.ds(k, 1)].reshape(rows, half)
 
     with jax.named_scope("n_inner"):
         lax.fori_loop(split, tiles, inner_tile, 0)
@@ -435,21 +490,46 @@
             for copy in rim_copies:
                 copy.wait_send()
 
-        for slot, d in group_sends:
-
-            @pl.when(sends_group(slot, d))
+        for shift in range(1, nx):
+            decay_to_owner(shift).wait_send()
+            for part in range(2):
+                to_owner(part, shift).wait_send()
+
+        @pl.when(jnp.logical_not(owner))
+        def _():
+            decay_to_owner(0).wait_send()
+            for part in range(2):
+                to_owner(part, 0).wait_send()
+
+        @pl.when(owner)
+        def _():
+            for slot, d in group_sends:
+
+                @pl.when(sends_group(slot, d))
+                def _():
+                    for copy in group_copies(slot, d):
+                        copy.wait_send()
+
+            for part in range(2):
+                for d in range(1, plane):
+                    back_copy(part, d).wait_send()
+
+        for part in range(2):
+
+            @pl.when(jnp.logical_not(owner))
             def _():
-                for copy in group_copies(slot, d):
-                    copy.wait_send()
-
-        for copy in back:
-            copy.wait()
+                back_from(part, 0).wait_recv()
+
+            for shift in range(1, nx):
+                back_from(part, shift).wait_recv()
 
     with jax.named_scope("p_outer"):
         squares = jnp.zeros((tok, 128), F32)
         for tile in range(tiles):
             lanes = slice(tile * 128, tile * 128 + 128)
-            gated = yg[:, lanes] + eg[:, lanes] * dot(cmat[...], ent[:, lanes])
+            part, begin = divmod(tile * 128, half)
+            outer = dot(cmat[...], ent[part, :, begin : begin + 128])
+            gated = yg[:, lanes] + eg[:, lanes] * outer
             yg[:, lanes] = gated
             squares = squares + gated * gated
 
@@ -465,11 +545,14 @@
         ]
         for copy in shared:
             copy.start()
-        for d in range(last_size, 0, -1):
-
-            @pl.when(sends_chain(d))
-            def _():
-                chain_copy(d).wait_send()
+        @pl.when(owner)
+        def _():
+            for d in range(last_size, 0, -1):
+
+                @pl.when(sends_chain(d))
+                def _():
+                    for part in range(2):
+                        chain_copy(part, d).wait_send()
 
         for copy in shared:
             copy.wait()
@@ -503,7 +586,7 @@
     tok, inner = x_in.shape
     heads = dt_raw.shape[0]
     plane = nx * nc
-    rows = STATE // plane
+    rows = STATE // nx
     half = inner // 2
     sizes = (nz, nx, nc, ny, tok, heads, inner)
     operands = (
@@ -523,19 +606,19 @@
         v((128, tok), F32), v((16, 128), F32),
         v((128, tok), F32), v((128, tok), F32), v((tok, 256), BF16), v((tok, 256), BF16),
         v((tok, 384), BF16), v((tok, inner), F32), v((tok, inner), F32), v((tok, inner), F32),
-        v((2, plane, rows, half), BF16), v((2, plane, rows, half), BF16), v((8, 128), F32),
+        v((2, nx, rows, half), BF16), v((2, plane, rows, half), BF16), v((8, 128), F32),
         v((plane, 8, 128), F32), v((plane, rows, inner), F32), v((plane, inner), F32),
         v((rows, inner), BF16), v((8, 128), F32), v((last - 1, rows, inner), BF16),
         v((last - 1, 8, 128), F32),
         v((rows, inner), F32), v((8, inner), F32), v((rows, inner), F32), v((8, inner), F32),
-        v((rows, inner), BF16), v((rows, inner), BF16),
-        v((plane, rows, inner), BF16), v((STATE, inner), BF16),
+        v((2, rows, half), BF16), v((2, rows, half), BF16),
+        v((2, plane, rows, half), BF16), v((2, STATE, half), BF16),
         v((8, tok), F32), v((others, 8, tok), F32),
         dma((11,)), dma((2,)), dma((2,)),
-        dma((2, plane - 1)), dma((2, plane - 1)), dma((plane - 1,)), dma((plane - 1,)),
+        dma((2, nx)), dma((2, plane)), dma((nx,)), dma((plane,)),
         dma((last - 1,)), dma((last - 1,)), dma((last - 1,)), dma((last - 1,)),
-        dma((last,)), dma((1,)),
-        dma((plane - 1,)), dma((plane - 1,)), dma((others,)), dma((others,)),
+        dma((2, last)), dma((2,)),
+        dma((2, plane - 1)), dma((2, nx)), dma((others,)), dma((others,)),
         pltpu.SemaphoreType.REGULAR((last,)),
     ]
     return pl.pallas_call(

time: 41.6 us -> 40 us (0.962); the launches traced: 41.5 us -> 39.4 us
  Pallas kernels: 40.6 us -> 38.6 us
    pallas_call x1, Pallas kernels: 40.6 us -> 38.6 us  [local(): pl.pallas_call(functools.partial(layer_kernel, sizes), out_shape=pltpu.VM...]
where the time goes in v3:
time: 40 us; the launch traced here: 39.4 us
  Pallas kernels  38.6 us (96%)
  local copies, waits for them, and re-layouts  0.84 us (2%)
    pallas_call x1, Pallas kernels, local(): pl.pallas_call(functools.partial(layer_kernel, sizes), out_shape=pltpu.VM...  38.6 us
    unnamed x1, local copies, waits for them, and re-layouts  0.84 us

profile of v3, /device:TPU:480, one launch (start us, length us, event | category | flops | bytes accessed | tf_op | source)
XLA Modules:
  0.0 39.4 jit_solution(7002608226100744264)
XLA Ops:
  0.0 38.6 %layer.1 = bf16[256,1280]{1,0:T(8,128)(2,1)S(1)} custom-call(bf16[256,1280]{1,0:T(8,128)(2,1)} %refs_0_.1, bf16[256,256]{1,0:T(8,128)(2,1)} %refs_1_.1, bf16[256,1280]{1,0:T(8,128)(2,1)} %refs_2_.1, f32[20,256]{1,0:T(8,128)} %refs_3_.1, f32[20]{0:T(128)} %refs_4_.1, f32[20]{0:T(128)} %refs_5_.1, f32[4,1280]{1,0:T(4,128)} %refs_6_.1, f32[4,256]{1,0:T(4,128)} %refs_7_.1, ...), custom_call_target="tpu_custom_call" | custom-call | tf_op jit(solution)/shard_map/layer/pallas_call | solution.py:624
  38.6 0.8 %copy.13 = bf16[256,1280]{1,0:T(8,128)(2,1)} copy(bf16[256,1280]{1,0:T(8,128)(2,1)S(1)} %layer.1) | data formatting | bytes 1310720
